TPU v7x, 128 devices: a whole 4x4x4 slice. The times are simulated.
128 devices in a mesh: pb: 16 (over z, y_hi, core), ka: 8 (over x, y_lo).
Axes of the slice: x: 4, y: 4 (y_hi: 2, y_lo: 2; y = y_hi * 2 + y_lo), z: 4, core: 2. Of those that a mesh axis runs over, the one named last changes fastest.
Arguments:
- activations: bfloat16 [4, 4096, 768], P(None, ('pb', 'ka')), may hold values from -6 to 6
- attn_gain: float32 [768], replicated, may hold values from 0.1 to 1.9
- w_qkv: bfloat16 [768, 2304], replicated, may hold values from -0.21875 to 0.21875
- w_gate: bfloat16 [768, 768], replicated, may hold values from -0.21875 to 0.21875
- w_out: bfloat16 [768, 768], replicated, may hold values from -0.21875 to 0.21875
- pair_bias: bfloat16 [16, 4096, 4096], P(None, 'pb', 'ka'), may hold values from -240 to 240
- chain_ids: int32 [4096], replicated, may hold values from 0 to 5, as said below
- binder_flag: int32 [4096], replicated, may hold values from 0 to 1, as said below
- trans_gain: float32 [768], replicated, may hold values from 0.1 to 1.9
- w_up: bfloat16 [768, 3072], replicated, may hold values from -0.21875 to 0.21875
- w_down: bfloat16 [1536, 768], replicated, may hold values from -0.15625 to 0.15625
Outputs:
- updated: bfloat16 [4, 4096, 768], P(None, ('pb', 'ka'))
Inputs may be any that keep to these rules, and one draw needn't show every extreme that they name: `chain_ids`: chain ids never fall along the tokens; every chain has at least one token. `binder_flag`: all tokens of one chain carry the same flag.
All inputs are finite; a program needn't handle non-finite values.
Results may differ from a plain program's by a relative error of at most 0.0056.
Values may be sent and summed in bfloat16 or wider, within the bound.
A program may use at most 128 MiB of HBM per device.

v0:
```python
import math
import jax
import jax.numpy as jnp
from jax import lax
from jax.sharding import PartitionSpec as P

epsilon = 1e-05
masked_score = -1000000000.0


def in_one_piece(arrays, axis, dim, along):
    ends, at = ([], 0)
    for a in arrays[:-1]:
        at += a.shape[along]
        ends.append(at)
    both = jnp.concatenate(arrays, axis=along)
    return tuple(jnp.split(lax.all_gather(both, axis, axis=dim, tiled=True), ends, axis=along))


def spread_2(value, axis, source):
    kept = jnp.where(lax.axis_index(axis) == source, value, 0).astype(value.dtype)
    return lax.psum(kept, axis)


def layer_norm(values, scales):
    centred = values - jnp.mean(values, axis=-1, keepdims=True)
    spread = jnp.mean(centred * centred, axis=-1, keepdims=True)
    return centred * lax.rsqrt(spread + epsilon) * scales


def block_stats(query_rows, key_block, value_block, bias_tile, allowed):
    head_count = bias_tile.shape[0]
    query_heads = query_rows.reshape(query_rows.shape[0], head_count, -1)
    key_heads = key_block.reshape(key_block.shape[0], head_count, -1)
    value_heads = value_block.reshape(value_block.shape[0], head_count, -1)
    head_size = query_heads.shape[-1]
    scores = jnp.einsum(
        "qhd,khd->hqk", query_heads, key_heads, preferred_element_type=jnp.float32
    ) / math.sqrt(head_size)
    scores = scores + bias_tile.astype(jnp.float32)
    best_score = jnp.max(jnp.where(allowed[None], scores, masked_score), axis=-1)
    weights = jnp.where(allowed[None], jnp.exp(scores - best_score[..., None]), 0.0)
    row_sum = jnp.sum(weights, axis=-1)
    block_out = jnp.einsum(
        "hqk,khd->qhd",
        weights.astype(jnp.bfloat16),
        value_heads,
        preferred_element_type=jnp.float32,
    )
    return (best_score.T, row_sum.T, block_out.reshape(query_rows.shape[0], -1))


def body(
    activations,
    attn_gain,
    w_qkv,
    w_gate,
    w_out,
    pair_bias,
    chain_ids,
    binder_flag,
    trans_gain,
    w_up,
    w_down,
):
    samples, own_rows, model_width = activations.shape
    head_count, query_count, key_count = pair_bias.shape
    pb_ratio = lax.axis_size("pb") // lax.axis_size("ka")
    normed = layer_norm(activations.astype(jnp.float32), attn_gain).astype(jnp.bfloat16)
    flat_normed = normed.reshape(-1, model_width)
    gate_pre = jnp.dot(flat_normed, w_gate, preferred_element_type=jnp.float32).reshape(
        samples, own_rows, model_width
    )
    queries = jnp.dot(flat_normed, w_qkv[:, :model_width], preferred_element_type=jnp.float32)
    queries = queries.astype(jnp.bfloat16).reshape(samples, own_rows, model_width)
    queries, block_normed = in_one_piece((queries, normed), "ka", 1, 0)
    input_parts = []
    for within in range(pb_ratio):
        source_index = lax.axis_index("ka") * pb_ratio + within
        input_parts.append(spread_2(block_normed, "pb", source_index))
    key_inputs = jnp.concatenate(input_parts, axis=1).reshape(-1, model_width)
    key_value = jnp.dot(key_inputs, w_qkv[:, model_width:], preferred_element_type=jnp.float32)
    key_block = (
        key_value[:, :model_width].astype(jnp.bfloat16).reshape(samples, key_count, model_width)
    )
    value_block = (
        key_value[:, model_width:].astype(jnp.bfloat16).reshape(samples, key_count, model_width)
    )
    query_start = lax.axis_index("pb") * query_count
    key_start = lax.axis_index("ka") * key_count
    row_chain = lax.dynamic_slice_in_dim(chain_ids, query_start, query_count, 0)
    row_binder = lax.dynamic_slice_in_dim(binder_flag, query_start, query_count, 0)
    col_chain = lax.dynamic_slice_in_dim(chain_ids, key_start, key_count, 0)
    col_binder = lax.dynamic_slice_in_dim(binder_flag, key_start, key_count, 0)
    allowed = (
        (row_binder[:, None] > 0)
        | (col_binder[None, :] > 0)
        | (row_chain[:, None] == col_chain[None, :])
    )

    def per_sample(operands):
        return block_stats(operands[0], operands[1], operands[2], pair_bias, allowed)

    block_tops, block_sums, block_outs = lax.map(per_sample, (queries, key_block, value_block))
    all_tops, all_sums, all_outs = (
        lax.all_to_all(block_tops[None], "ka", split_axis=2, concat_axis=0, tiled=True),
        lax.all_to_all(block_sums[None], "ka", split_axis=2, concat_axis=0, tiled=True),
        lax.all_to_all(block_outs[None], "ka", split_axis=2, concat_axis=0, tiled=True),
    )
    overall = jnp.max(all_tops, axis=0)
    factors = jnp.exp(all_tops - overall)
    row_sum = jnp.sum(factors * all_sums, axis=0)
    shaped = all_outs.reshape(all_outs.shape[:-1] + (head_count, -1))
    row_out = jnp.sum(factors[..., None] * shaped, axis=0).reshape(samples, own_rows, model_width)
    attention = (row_out.reshape(samples, own_rows, head_count, -1) / row_sum[..., None]).reshape(
        samples, own_rows, model_width
    )
    gated = (jax.nn.sigmoid(gate_pre) * attention).astype(jnp.bfloat16)
    mixed = activations.astype(jnp.float32) + jnp.dot(
        gated.reshape(-1, model_width), w_out, preferred_element_type=jnp.float32
    ).reshape(samples, own_rows, model_width)
    trans_normed = layer_norm(mixed, trans_gain).astype(jnp.bfloat16)
    both_parts = jnp.dot(
        trans_normed.reshape(-1, model_width), w_up, preferred_element_type=jnp.float32
    )
    hidden_width = w_down.shape[0]
    hidden = (jax.nn.silu(both_parts[:, :hidden_width]) * both_parts[:, hidden_width:]).astype(
        jnp.bfloat16
    )
    updated = mixed + jnp.dot(hidden, w_down, preferred_element_type=jnp.float32).reshape(
        samples, own_rows, model_width
    )
    return updated.astype(jnp.bfloat16)


def solution(mesh):
    placed = (
        P(None, ("pb", "ka"), None),
        P(),
        P(),
        P(),
        P(),
        P(None, "pb", "ka"),
        P(),
        P(),
        P(),
        P(),
        P(),
    )
    return jax.shard_map(
        body, mesh=mesh, in_specs=placed, out_specs=P(None, ("pb", "ka"), None), check_vma=False
    )
```

profile of v0, /device:TPU:121, one launch (start us, length us, event | category | flops | bytes accessed | tf_op | source)
XLA Modules:
  0.0 497.9 jit_solution(10470582669954090714)
XLA Ops:
  6.5 1.2 convert_reduce_fusion
  10.0 1.6 fusion.22
  12.4 70.0 %all-gather.2.cloned.1.call-done = bf16[8,256,768]{2,1,0:T(8,128)(2,1)} async-done(((bf16[8,32,768]{2,1,0:T(8,128)(2,1)}), bf16[8,256,768]{2,1,0:T(8,128)(2,1)}) %all-gather.2.cloned.1.call-update) | async-done | bytes 3145744 | tf_op jit(solution)/shard_map/all_gather | solution.py:17
  82.5 4.2 broadcast_select_fusion.1
  89.7 150.4 %all-reduce.3.cloned.1.call-done = (bf16[4,256,768]{2,1,0:T(8,128)(2,1)}, bf16[4,256,768]{2,1,0:T(8,128)(2,1)}) async-done(((bf16[4,256,768]{2,1,0:T(8,128)(2,1)}, bf16[4,256,768]{2,1,0:T(8,128)(2,1)}), (bf16[4,256,768]{2,1,0:T(8,128)(2,1)}, bf16[4,256,768]{2,1,0:T(8,128)(2,1)})) %all-reduce.3.cloned.1.call-update) | async-done | bytes 3145744 | tf_op jit(solution)/shard_map/psum | solution.py:22
  240.2 2.2 pad_maximum_fusion
  243.1 5.4 %convolution_convert_fusion = bf16[2048,1536]{1,0:T(8,128)(2,1)S(1)} fusion(bf16[2048,768]{1,0:T(8,128)(2,1)S(1)} %bitcast.103, bf16[768,2304]{1,0:T(8,128)(2,1)S(1)} %copy-done.6), kind=kOutput, calls=%fused_computation.17 | convolution fusion | flops 4834983936 | bytes 11796480 | tf_op jit(solution)/shard_map/dot_general | solution.py:82
  248.5 3.1 fusion.45
  251.6 158.6 %while.15 = (s32[]{:T(128)}, f32[4,256,16]{1,2,0:T(8,128)S(1)}, f32[4,256,16]{1,2,0:T(8,128)S(1)}, f32[4,256,768]{2,0,1:T(4,128)}, bf16[4,256,768]{2,1,0:T(8,128...) while((s32[]{:T(128)}, f32[4,256,16]{1,2,0:T(8,128)S(1)}, ...), condition=%wide.region_7.8_spmd.clone, body=%wide.region_4.7_spmd.clone.sunk | while | flops 426106880 | bytes 77336504 | solution.py:104
  256.1 4.9 select_reduce_fusion.2
  261.0 2.4 fusion.70
  264.2 2.1 constant_dynamic-slice_fusion.8
  266.3 1.4 copy.48
  267.7 5.8 %fusion.71 = f32[16,48,256]{2,1,0:T(8,128)} fusion(bf16[512,16,48]{0,2,1:T(8,128)(2,1)S(1)} %bitcast.95, f32[16,256,512]{2,1,0:T(8,128)} %copy-done.1, f32[16,256]{1,0:T(8,128)S(1)} %get-tuple-element.240, pred[256,512]{1,0:T(8,128)(4,1)S(1)} %compare_or_fusion.2), kind=kOutput, calls=%fused_computation.6.clone.1 | convolution fusion | flops 207618048 | bytes 10108928 | tf_op jit(solution)/shard_map/while/body/eval_jaxpr/hqk,khd->qhd/dot_general | solution.py:44
  273.5 2.3 copy.49
  275.8 15.4 %dynamic_update_slice.19 = f32[4,256,768]{2,0,1:T(4,128)} dynamic-update-slice(f32[4,256,768]{2,0,1:T(4,128)} %get-tuple-element.260, f32[1,256,768]{2,0,1:T(1,128)S(1)} %copy.49, s32[]{:T(128)S(6)} %copy.59, s32[]{:T(128)} %constant.36.clone.1..sunk, s32[]{:T(128)} %constant.36.clone.1..sunk) | dynamic-update-slice | bytes 1572868 | tf_op jit(solution)/shard_map/while/body/jit(dynamic_update_index_in_dim)/dynamic_update_slice | solution.py:104
  295.7 4.9 select_reduce_fusion.2
  300.6 2.4 fusion.70
  303.8 2.1 constant_dynamic-slice_fusion.8
  305.9 1.4 copy.48
  307.3 5.8 %fusion.71 = f32[16,48,256]{2,1,0:T(8,128)} fusion(bf16[512,16,48]{0,2,1:T(8,128)(2,1)S(1)} %bitcast.95, f32[16,256,512]{2,1,0:T(8,128)} %copy-done.1, f32[16,256]{1,0:T(8,128)S(1)} %get-tuple-element.240, pred[256,512]{1,0:T(8,128)(4,1)S(1)} %compare_or_fusion.2), kind=kOutput, calls=%fused_computation.6.clone.1 | convolution fusion | flops 207618048 | bytes 10108928 | tf_op jit(solution)/shard_map/while/body/eval_jaxpr/hqk,khd->qhd/dot_general | solution.py:44
  313.2 2.3 copy.49
  315.5 15.4 %dynamic_update_slice.19 = f32[4,256,768]{2,0,1:T(4,128)} dynamic-update-slice(f32[4,256,768]{2,0,1:T(4,128)} %get-tuple-element.260, f32[1,256,768]{2,0,1:T(1,128)S(1)} %copy.49, s32[]{:T(128)S(6)} %copy.59, s32[]{:T(128)} %constant.36.clone.1..sunk, s32[]{:T(128)} %constant.36.clone.1..sunk) | dynamic-update-slice | bytes 1572868 | tf_op jit(solution)/shard_map/while/body/jit(dynamic_update_index_in_dim)/dynamic_update_slice | solution.py:104
  333.1 1.2 constant_dynamic-slice_fusion.7
  335.4 4.9 select_reduce_fusion.2
  340.3 2.4 fusion.70
  343.5 2.1 constant_dynamic-slice_fusion.8
  345.6 1.4 copy.48
  347.0 5.8 %fusion.71 = f32[16,48,256]{2,1,0:T(8,128)} fusion(bf16[512,16,48]{0,2,1:T(8,128)(2,1)S(1)} %bitcast.95, f32[16,256,512]{2,1,0:T(8,128)} %copy-done.1, f32[16,256]{1,0:T(8,128)S(1)} %get-tuple-element.240, pred[256,512]{1,0:T(8,128)(4,1)S(1)} %compare_or_fusion.2), kind=kOutput, calls=%fused_computation.6.clone.1 | convolution fusion | flops 207618048 | bytes 10108928 | tf_op jit(solution)/shard_map/while/body/eval_jaxpr/hqk,khd->qhd/dot_general | solution.py:44
  352.8 2.3 copy.49
  355.1 15.4 %dynamic_update_slice.19 = f32[4,256,768]{2,0,1:T(4,128)} dynamic-update-slice(f32[4,256,768]{2,0,1:T(4,128)} %get-tuple-element.260, f32[1,256,768]{2,0,1:T(1,128)S(1)} %copy.49, s32[]{:T(128)S(6)} %copy.59, s32[]{:T(128)} %constant.36.clone.1..sunk, s32[]{:T(128)} %constant.36.clone.1..sunk) | dynamic-update-slice | bytes 1572868 | tf_op jit(solution)/shard_map/while/body/jit(dynamic_update_index_in_dim)/dynamic_update_slice | solution.py:104
  375.1 4.9 select_reduce_fusion.2
  379.9 2.4 fusion.70
  383.2 2.1 constant_dynamic-slice_fusion.8
  385.2 1.4 copy.48
  386.7 5.8 %fusion.71 = f32[16,48,256]{2,1,0:T(8,128)} fusion(bf16[512,16,48]{0,2,1:T(8,128)(2,1)S(1)} %bitcast.95, f32[16,256,512]{2,1,0:T(8,128)} %copy-done.1, f32[16,256]{1,0:T(8,128)S(1)} %get-tuple-element.240, pred[256,512]{1,0:T(8,128)(4,1)S(1)} %compare_or_fusion.2), kind=kOutput, calls=%fused_computation.6.clone.1 | convolution fusion | flops 207618048 | bytes 10108928 | tf_op jit(solution)/shard_map/while/body/eval_jaxpr/hqk,khd->qhd/dot_general | solution.py:44
  392.5 2.3 copy.49
  394.8 15.4 %dynamic_update_slice.19 = f32[4,256,768]{2,0,1:T(4,128)} dynamic-update-slice(f32[4,256,768]{2,0,1:T(4,128)} %get-tuple-element.260, f32[1,256,768]{2,0,1:T(1,128)S(1)} %copy.49, s32[]{:T(128)S(6)} %copy.59, s32[]{:T(128)} %constant.36.clone.1..sunk, s32[]{:T(128)} %constant.36.clone.1..sunk) | dynamic-update-slice | bytes 1572868 | tf_op jit(solution)/shard_map/while/body/jit(dynamic_update_index_in_dim)/dynamic_update_slice | solution.py:104
  411.6 5.2 %all-to-all-start.2 = ((f32[8,1,2048]{2,1,0:T(1,128)}), f32[8,1,2048]{2,1,0:T(1,128)S(1)}, u32[]{:S(2)}, u32[]{:S(2)}) async-start(f32[8,1,2048]{2,1,0:T(1,128)} %reshape.108), calls=%async_computation.2 | async-start | bytes 131072 | tf_op jit(solution)/shard_map/all_to_all | solution.py:107
  417.5 3.5 all-to-all-done.2
  420.9 7.7 %all_to_all.51 = f32[8,1,2048]{2,1,0:T(1,128)S(1)} all-to-all(f32[8,1,2048]{2,1,0:T(1,128)S(1)} %reshape.106), channel_id=1, replica_groups=mesh['pb'=16,'ka'=8] {'ka'}, dimensions={0} | all-to-all | bytes 131072 | tf_op jit(solution)/shard_map/all_to_all | solution.py:106
  428.6 5.3 %all-to-all-start.1 = ((f32[1,4,256,768]{3,1,0,2:T(4,128)}), f32[1,4,256,768]{3,1,0,2:T(4,128)}, u32[]{:S(2)}, u32[]{:S(2)}) async-start(f32[1,4,256,768]{3,1,0,2:T(4,128)} %bitcast.102), calls=%async_computation.1 | async-start | bytes 6291456 | tf_op jit(solution)/shard_map/all_to_all | solution.py:108
  437.7 4.6 mul.80
  442.2 7.7 %mul.81 = f32[8,1,4,32,768]{4,3,0,2,1:T(8,128)} reshape(f32[8,4,32,16,48]{4,3,2,0,1:T(8,128)} %mul.80) | data formatting | bytes 6291456 | tf_op jit(solution)/shard_map/mul | solution.py:114
  451.5 28.4 %all-to-all-done.1 = f32[1,4,256,768]{3,1,0,2:T(4,128)} async-done(((f32[1,4,256,768]{3,1,0,2:T(4,128)}), f32[1,4,256,768]{3,1,0,2:T(4,128)}, u32[]{:S(2)}, u32[]{:S(2)}) %all-to-all-start.1) | async-done | bytes 3145760 | tf_op jit(solution)/shard_map/all_to_all | solution.py:108
  479.9 2.6 copy.27
  483.7 2.5 fusion.46
  486.6 3.1 fusion.51
  (85 shorter events, 36.9 us)
Async XLA Ops:
  6.5 483.2 %copy-start = (bf16[1536,768]{1,0:T(8,128)(2,1)S(1)}, bf16[1536,768]{1,0:T(8,128)(2,1)}, u32[]{:S(2)}) copy-start(bf16[1536,768]{1,0:T(8,128)(2,1)} %param.23) | copy-start | bytes 7077892
  6.5 75.9 %all-gather.2.cloned.1.call-start = ((), (), s32[]{:S(2)}) async-start(), calls=%async_computation.3 | async-start | bytes 3538944 | tf_op jit(solution)/shard_map/all_gather | solution.py:17
  12.4 227.8 %all-reduce.3.cloned.1.call-start = ((), (), s32[]{:S(2)}) async-start(), calls=%async_computation.4 | async-start | bytes 6291456 | tf_op jit(solution)/shard_map/psum | solution.py:22
  240.2 2.9 copy-start.6
  261.0 3.2 copy-start.1
  300.6 3.2 copy-start.1
  340.3 3.2 copy-start.1
  379.9 3.2 copy-start.1
  411.6 9.3 %all-to-all-start.2 = ((f32[8,1,2048]{2,1,0:T(1,128)}), f32[8,1,2048]{2,1,0:T(1,128)S(1)}, u32[]{:S(2)}, u32[]{:S(2)}) async-start(f32[8,1,2048]{2,1,0:T(1,128)} %reshape.108), calls=%async_computation.2 | async-start | bytes 131072 | tf_op jit(solution)/shard_map/all_to_all | solution.py:107
  428.6 51.3 %all-to-all-start.1 = ((f32[1,4,256,768]{3,1,0,2:T(4,128)}), f32[1,4,256,768]{3,1,0,2:T(4,128)}, u32[]{:S(2)}, u32[]{:S(2)}) async-start(f32[1,4,256,768]{3,1,0,2:T(4,128)} %bitcast.102), calls=%async_computation.1 | async-start | bytes 6291456 | tf_op jit(solution)/shard_map/all_to_all | solution.py:108
  479.9 2.8 copy-start.2
  482.8 0.9 copy-start.3
  482.8 0.9 copy-start.4
  483.7 2.8 copy-start.5
Sparse Core Ops, SparseCore 0:
  12.5 69.9 all-gather.1
  86.8 153.3 all-reduce.2
where the time goes:
time: 501 us; the launch traced here: 498 us
  waiting for transfers between devices  252 us (50%)
  local copies, waits for them, and re-layouts  132 us (26%)
  matrix products  56.1 us (11%)
  other arithmetic  25.7 us (5%)
  between operations  13.7 us (3%)
  starting transfers between devices  10.5 us (2%)
  blocking collectives  7.65 us (2%)
    psum x1, waiting for transfers between devices, spread_2(): return lax.psum(kept, axis)  150 us
    dynamic_update_slice x12, local copies, waits for them, and re-layouts, body(): lax.map(per_sample, (queries, key_block, value_block))  71 us
    all_gather x1, waiting for transfers between devices, in_one_piece(): lax.all_gather(both, axis, axis=dim, tiled=True)  70 us
    dynamic_slice x24, local copies, waits for them, and re-layouts, body(): lax.map(per_sample, (queries, key_block, value_block))  31.1 us
    all_to_all x1, waiting for transfers between devices, body(): lax.all_to_all(block_outs[None], 'ka', split_axis=2, concat_axis=0, tiled...  28.4 us
    dot_general x4, matrix products, block_stats(): jnp.einsum('hqk,khd->qhd', weights.astype(jnp.bfloat16), value_heads, pre...  23.3 us
    dot_general x4, matrix products, block_stats(): jnp.einsum('qhd,khd->hqk', query_heads, key_heads, preferred_element_type...  19.5 us
    mul x2, local copies, waits for them, and re-layouts, body(): factors[..., None] * shaped  12.3 us
  transfers between devices with their start and end apart: 4, of which 4 were waited for; matrix products, arithmetic and copies ran while one was open for 4% of the time, Pallas kernels for 0%

commit v1 on v0

--- a/solution.py
+++ b/solution.py
@@ -6,6 +6,13 @@
 
 epsilon = 1e-05
 masked_score = -1000000000.0
+
+
+def swap_blocks(x, name, split, join):
+    devices = lax.axis_size(name)
+    shards = jnp.stack(jnp.split(x, devices, axis=split), axis=0)
+    shards = lax.all_to_all(shards, name, split_axis=0, concat_axis=0)
+    return jnp.concatenate(shards, axis=join)
 
 
 def in_one_piece(arrays, axis, dim, along):
@@ -105,7 +112,7 @@
     all_tops, all_sums, all_outs = (
         lax.all_to_all(block_tops[None], "ka", split_axis=2, concat_axis=0, tiled=True),
         lax.all_to_all(block_sums[None], "ka", split_axis=2, concat_axis=0, tiled=True),
-        lax.all_to_all(block_outs[None], "ka", split_axis=2, concat_axis=0, tiled=True),
+        swap_blocks(block_outs[None], "ka", 2, 0),
     )
     overall = jnp.max(all_tops, axis=0)
     factors = jnp.exp(all_tops - overall)

time: 501 us -> 444 us (0.89)
  local copies, waits for them, and re-layouts: 132 us -> 78.5 us
  blocking collectives: 7.65 us -> 0 us
  starting transfers between devices: 10.5 us -> 15.8 us
    dynamic_update_slice x12, local copies, waits for them, and re-layouts: 71 us -> 9.39 us  [body(): lax.map(per_sample, (queries, key_block, value_block))]
    unnamed x18 -> x25, local copies, waits for them, and re-layouts: 3.55 us -> 12.3 us
    all_to_all x1 -> x0, blocking collectives: 7.65 us -> none  [body(): lax.all_to_all(block_tops[None], 'ka', split_axis=2, concat_axis=0, tiled...]
    all_to_all x1 -> x2, starting transfers between devices: 5.28 us -> 10.6 us  [the longest x1 5.32 us: body(): lax.all_to_all(block_tops[None], 'ka', split_axis=2, concat_axis=0, tiled...]
    all_to_all x1 -> x2, waiting for transfers between devices: 28.4 us -> 29.5 us  [the longest x1 27.1 us: swap_blocks(): shards = lax.all_to_all(shards, name, split_axis=0, concat_axis=0)]
  transfers between devices with their start and end apart: 4 -> 5, of which waited for: 4 -> 4; matrix products, arithmetic and copies ran while one was open for 4% -> 7% of each run, Pallas kernels for 0% -> 0%
where the time goes in v1:
time: 444 us; the launch traced here: 443 us
  waiting for transfers between devices  250 us (56%)
  local copies, waits for them, and re-layouts  78.5 us (18%)
  matrix products  56.1 us (13%)
  other arithmetic  28.4 us (6%)
  starting transfers between devices  15.8 us (4%)
  between operations  13.7 us (3%)
    psum x1, waiting for transfers between devices, spread_2(): return lax.psum(kept, axis)  150 us
    all_gather x1, waiting for transfers between devices, in_one_piece(): lax.all_gather(both, axis, axis=dim, tiled=True)  70 us
    dynamic_slice x24, local copies, waits for them, and re-layouts, body(): lax.map(per_sample, (queries, key_block, value_block))  31.2 us
    all_to_all x1, waiting for transfers between devices, swap_blocks(): shards = lax.all_to_all(shards, name, split_axis=0, concat_axis=0)  27.1 us
    dot_general x4, matrix products, block_stats(): jnp.einsum('hqk,khd->qhd', weights.astype(jnp.bfloat16), value_heads, pre...  23.3 us
    dot_general x4, matrix products, block_stats(): jnp.einsum('qhd,khd->hqk', query_heads, key_heads, preferred_element_type...  19.5 us
    mul x2, local copies, waits for them, and re-layouts, body(): factors[..., None] * shaped  12.3 us
    unnamed x25, local copies, waits for them, and re-layouts  12.3 us
  transfers between devices with their start and end apart: 5, of which 4 were waited for; matrix products, arithmetic and copies ran while one was open for 7% of the time, Pallas kernels for 0%

profile of v1, /device:TPU:121, one launch (start us, length us, event | category | flops | bytes accessed | tf_op | source)
XLA Modules:
  0.0 442.6 jit_solution(17811978237152378318)
XLA Ops:
  10.0 1.6 fusion.22
  12.4 70.0 %all-gather.2.cloned.1.call-done = bf16[8,256,768]{2,1,0:T(8,128)(2,1)} async-done(((bf16[8,32,768]{2,1,0:T(8,128)(2,1)}), bf16[8,256,768]{2,1,0:T(8,128)(2,1)}) %all-gather.2.cloned.1.call-update) | async-done | bytes 3145744 | tf_op jit(solution)/shard_map/all_gather | solution.py:24
  82.5 4.2 broadcast_select_fusion.1
  89.8 150.4 %all-reduce.3.cloned.1.call-done = (bf16[4,256,768]{2,1,0:T(8,128)(2,1)}, bf16[4,256,768]{2,1,0:T(8,128)(2,1)}) async-done(((bf16[4,256,768]{2,1,0:T(8,128)(2,1)}, bf16[4,256,768]{2,1,0:T(8,128)(2,1)}), (bf16[4,256,768]{2,1,0:T(8,128)(2,1)}, bf16[4,256,768]{2,1,0:T(8,128)(2,1)})) %all-reduce.3.cloned.1.call-update) | async-done | bytes 3145744 | tf_op jit(solution)/shard_map/psum | solution.py:29
  240.2 2.2 pad_maximum_fusion
  243.1 5.4 %convolution_convert_fusion = bf16[2048,1536]{1,0:T(8,128)(2,1)S(1)} fusion(bf16[2048,768]{1,0:T(8,128)(2,1)S(1)} %bitcast.136, bf16[768,2304]{1,0:T(8,128)(2,1)S(1)} %copy-done.6), kind=kOutput, calls=%fused_computation.18 | convolution fusion | flops 4834983936 | bytes 11796480 | tf_op jit(solution)/shard_map/dot_general | solution.py:89
  248.5 3.1 fusion.53
  251.6 97.4 %while.15 = (s32[]{:T(128)}, f32[4,256,16]{1,2,0:T(8,128)S(1)}, f32[4,256,16]{1,2,0:T(8,128)S(1)}, f32[4,256,768]{2,1,0:T(8,128)}, bf16[4,256,768]{2,1,0:T(8,128...) while((s32[]{:T(128)}, f32[4,256,16]{1,2,0:T(8,128)S(1)}, ...), condition=%wide.region_7.8_spmd.clone, body=%wide.region_4.7_spmd.clone.sunk | while | flops 426106880 | bytes 77336496 | solution.py:111
  253.7 1.2 constant_dynamic-slice_fusion.7
  256.1 4.9 %select_reduce_fusion.2 = (f32[16,256]{1,0:T(8,128)S(1)}, f32[16,256,512]{2,1,0:T(8,128)S(1)}) fusion(pred[256,512]{1,0:T(8,128)(4,1)S(1)} %compare_or_fusion.2, bf16[16,256,512]{2,1,0:T(8,128)(2,1)} %get-tuple-element.275, bf16[256,16,48]{0,2,1:T(8,128)(2,1)} %bitcast.125, bf16[512,16,48]{0,2,1:T(8,128)(2,1)} %bitcast.124), kind=kOutput, calls=%fused_computation.2.clone.1 | convolution fusion | flops 211808256 | bytes 13910016 | tf_op jit(solution)/shard_map/while/body/eval_jaxpr/qhd,khd->hqk/dot_general | solution.py:44
  261.0 2.4 fusion.78
  264.3 2.1 constant_dynamic-slice_fusion.8
  266.4 1.4 copy.57
  267.8 5.8 %fusion.79 = f32[16,48,256]{2,1,0:T(8,128)} fusion(bf16[512,16,48]{0,2,1:T(8,128)(2,1)S(1)} %bitcast.122, f32[16,256,512]{2,1,0:T(8,128)} %copy-done.1, f32[16,256]{1,0:T(8,128)S(1)} %get-tuple-element.240, pred[256,512]{1,0:T(8,128)(4,1)S(1)} %compare_or_fusion.2), kind=kOutput, calls=%fused_computation.6.clone.1 | convolution fusion | flops 207618048 | bytes 10108928 | tf_op jit(solution)/shard_map/while/body/eval_jaxpr/hqk,khd->qhd/dot_general | solution.py:51
  273.6 1.4 copy.58
  278.1 1.2 constant_dynamic-slice_fusion.7
  280.4 4.9 %select_reduce_fusion.2 = (f32[16,256]{1,0:T(8,128)S(1)}, f32[16,256,512]{2,1,0:T(8,128)S(1)}) fusion(pred[256,512]{1,0:T(8,128)(4,1)S(1)} %compare_or_fusion.2, bf16[16,256,512]{2,1,0:T(8,128)(2,1)} %get-tuple-element.275, bf16[256,16,48]{0,2,1:T(8,128)(2,1)} %bitcast.125, bf16[512,16,48]{0,2,1:T(8,128)(2,1)} %bitcast.124), kind=kOutput, calls=%fused_computation.2.clone.1 | convolution fusion | flops 211808256 | bytes 13910016 | tf_op jit(solution)/shard_map/while/body/eval_jaxpr/qhd,khd->hqk/dot_general | solution.py:44
  285.3 2.4 fusion.78
  288.6 2.1 constant_dynamic-slice_fusion.8
  290.7 1.4 copy.57
  292.1 5.8 %fusion.79 = f32[16,48,256]{2,1,0:T(8,128)} fusion(bf16[512,16,48]{0,2,1:T(8,128)(2,1)S(1)} %bitcast.122, f32[16,256,512]{2,1,0:T(8,128)} %copy-done.1, f32[16,256]{1,0:T(8,128)S(1)} %get-tuple-element.240, pred[256,512]{1,0:T(8,128)(4,1)S(1)} %compare_or_fusion.2), kind=kOutput, calls=%fused_computation.6.clone.1 | convolution fusion | flops 207618048 | bytes 10108928 | tf_op jit(solution)/shard_map/while/body/eval_jaxpr/hqk,khd->qhd/dot_general | solution.py:51
  297.9 1.4 copy.58
  304.8 4.9 %select_reduce_fusion.2 = (f32[16,256]{1,0:T(8,128)S(1)}, f32[16,256,512]{2,1,0:T(8,128)S(1)}) fusion(pred[256,512]{1,0:T(8,128)(4,1)S(1)} %compare_or_fusion.2, bf16[16,256,512]{2,1,0:T(8,128)(2,1)} %get-tuple-element.275, bf16[256,16,48]{0,2,1:T(8,128)(2,1)} %bitcast.125, bf16[512,16,48]{0,2,1:T(8,128)(2,1)} %bitcast.124), kind=kOutput, calls=%fused_computation.2.clone.1 | convolution fusion | flops 211808256 | bytes 13910016 | tf_op jit(solution)/shard_map/while/body/eval_jaxpr/qhd,khd->hqk/dot_general | solution.py:44
  309.7 2.4 fusion.78
  313.0 2.1 constant_dynamic-slice_fusion.8
  315.1 1.4 copy.57
  316.5 5.8 %fusion.79 = f32[16,48,256]{2,1,0:T(8,128)} fusion(bf16[512,16,48]{0,2,1:T(8,128)(2,1)S(1)} %bitcast.122, f32[16,256,512]{2,1,0:T(8,128)} %copy-done.1, f32[16,256]{1,0:T(8,128)S(1)} %get-tuple-element.240, pred[256,512]{1,0:T(8,128)(4,1)S(1)} %compare_or_fusion.2), kind=kOutput, calls=%fused_computation.6.clone.1 | convolution fusion | flops 207618048 | bytes 10108928 | tf_op jit(solution)/shard_map/while/body/eval_jaxpr/hqk,khd->qhd/dot_general | solution.py:51
  322.3 1.4 copy.58
  329.2 4.9 %select_reduce_fusion.2 = (f32[16,256]{1,0:T(8,128)S(1)}, f32[16,256,512]{2,1,0:T(8,128)S(1)}) fusion(pred[256,512]{1,0:T(8,128)(4,1)S(1)} %compare_or_fusion.2, bf16[16,256,512]{2,1,0:T(8,128)(2,1)} %get-tuple-element.275, bf16[256,16,48]{0,2,1:T(8,128)(2,1)} %bitcast.125, bf16[512,16,48]{0,2,1:T(8,128)(2,1)} %bitcast.124), kind=kOutput, calls=%fused_computation.2.clone.1 | convolution fusion | flops 211808256 | bytes 13910016 | tf_op jit(solution)/shard_map/while/body/eval_jaxpr/qhd,khd->hqk/dot_general | solution.py:44
  334.0 2.4 fusion.78
  337.3 2.1 constant_dynamic-slice_fusion.8
  339.4 1.4 copy.57
  340.8 5.8 %fusion.79 = f32[16,48,256]{2,1,0:T(8,128)} fusion(bf16[512,16,48]{0,2,1:T(8,128)(2,1)S(1)} %bitcast.122, f32[16,256,512]{2,1,0:T(8,128)} %copy-done.1, f32[16,256]{1,0:T(8,128)S(1)} %get-tuple-element.240, pred[256,512]{1,0:T(8,128)(4,1)S(1)} %compare_or_fusion.2), kind=kOutput, calls=%fused_computation.6.clone.1 | convolution fusion | flops 207618048 | bytes 10108928 | tf_op jit(solution)/shard_map/while/body/eval_jaxpr/hqk,khd->qhd/dot_general | solution.py:51
  346.7 1.4 copy.58
  350.4 5.2 %all-to-all-start.2 = ((f32[8,1,2048]{2,1,0:T(1,128)}), f32[8,1,2048]{2,1,0:T(1,128)S(1)}, u32[]{:S(2)}, u32[]{:S(2)}) async-start(f32[8,1,2048]{2,1,0:T(1,128)} %reshape.106), calls=%async_computation.2 | async-start | bytes 131072 | tf_op jit(solution)/shard_map/all_to_all | solution.py:114
  355.8 1.9 fusion.42
  357.7 1.8 fusion.41
  359.5 1.8 fusion.40
  365.5 5.3 %all-to-all-start = ((f32[8,1,2048]{2,1,0:T(1,128)}), f32[8,1,2048]{2,1,0:T(1,128)S(1)}, u32[]{:S(2)}, u32[]{:S(2)}) async-start(f32[8,1,2048]{2,1,0:T(1,128)} %reshape.104), calls=%async_computation | async-start | bytes 131072 | tf_op jit(solution)/shard_map/all_to_all | solution.py:113
  370.8 1.8 fusion.35
  372.6 2.4 all-to-all-done
  375.0 5.2 %all-to-all-start.1 = ((f32[8,1,4,32,768]{4,3,2,1,0:T(8,128)}), f32[8,1,4,32,768]{4,3,2,1,0:T(8,128)}, u32[]{:S(2)}, u32[]{:S(2)}) async-start(f32[8,1,4,32,768]{4,3,2,1,0:T(8,128)} %fusion.35), calls=%async_computation.1 | async-start | bytes 6291456 | tf_op jit(solution)/shard_map/all_to_all | solution.py:14
  384.0 4.6 %mul.80 = f32[8,4,32,16,48]{4,3,2,1,0:T(8,128)} broadcast(f32[8,4,32,16]{3,2,1,0:T(8,128)S(1)} %copy.32), dimensions={0,1,2,3} | broadcast | bytes 3211264 | tf_op jit(solution)/shard_map/mul | solution.py:121
  388.6 7.7 %mul.81 = f32[8,1,4,32,768]{4,3,2,1,0:T(8,128)} reshape(f32[8,4,32,16,48]{4,3,2,1,0:T(8,128)} %mul.80) | data formatting | bytes 6291456 | tf_op jit(solution)/shard_map/mul | solution.py:121
  398.0 27.1 %all-to-all-done.1 = f32[8,1,4,32,768]{4,3,2,1,0:T(8,128)} async-done(((f32[8,1,4,32,768]{4,3,2,1,0:T(8,128)}), f32[8,1,4,32,768]{4,3,2,1,0:T(8,128)}, u32[]{:S(2)}, u32[]{:S(2)}) %all-to-all-start.1) | async-done | bytes 3145760 | tf_op jit(solution)/shard_map/all_to_all | solution.py:14
  425.1 3.3 multiply_reduce_fusion
  428.4 2.5 fusion.54
  431.3 3.2 fusion.59
  (93 shorter events, 43.8 us)
Async XLA Ops:
  6.5 427.9 %copy-start = (bf16[1536,768]{1,0:T(8,128)(2,1)S(1)}, bf16[1536,768]{1,0:T(8,128)(2,1)}, u32[]{:S(2)}) copy-start(bf16[1536,768]{1,0:T(8,128)(2,1)} %param.23) | copy-start | bytes 7077892
  6.5 75.9 %all-gather.2.cloned.1.call-start = ((), (), s32[]{:S(2)}) async-start(), calls=%async_computation.3 | async-start | bytes 3538944 | tf_op jit(solution)/shard_map/all_gather | solution.py:24
  12.4 227.8 %all-reduce.3.cloned.1.call-start = ((), (), s32[]{:S(2)}) async-start(), calls=%async_computation.4 | async-start | bytes 6291456 | tf_op jit(solution)/shard_map/psum | solution.py:29
  240.2 2.9 copy-start.6
  261.0 3.3 copy-start.1
  285.3 3.3 copy-start.1
  309.7 3.3 copy-start.1
  334.0 3.3 copy-start.1
  350.4 15.1 %all-to-all-start.2 = ((f32[8,1,2048]{2,1,0:T(1,128)}), f32[8,1,2048]{2,1,0:T(1,128)S(1)}, u32[]{:S(2)}, u32[]{:S(2)}) async-start(f32[8,1,2048]{2,1,0:T(1,128)} %reshape.106), calls=%async_computation.2 | async-start | bytes 131072 | tf_op jit(solution)/shard_map/all_to_all | solution.py:114
  355.8 5.5 %copy-start.2 = (f32[4,256,768]{2,1,0:T(8,128)S(1)}, f32[4,256,768]{2,1,0:T(8,128)}, u32[]{:S(2)}) copy-start(f32[4,256,768]{2,1,0:T(8,128)} %get-tuple-element.55) | copy-start | bytes 9437188
  365.5 9.5 %all-to-all-start = ((f32[8,1,2048]{2,1,0:T(1,128)}), f32[8,1,2048]{2,1,0:T(1,128)S(1)}, u32[]{:S(2)}, u32[]{:S(2)}) async-start(f32[8,1,2048]{2,1,0:T(1,128)} %reshape.104), calls=%async_computation | async-start | bytes 131072 | tf_op jit(solution)/shard_map/all_to_all | solution.py:113
  375.0 50.1 %all-to-all-start.1 = ((f32[8,1,4,32,768]{4,3,2,1,0:T(8,128)}), f32[8,1,4,32,768]{4,3,2,1,0:T(8,128)}, u32[]{:S(2)}, u32[]{:S(2)}) async-start(f32[8,1,4,32,768]{4,3,2,1,0:T(8,128)} %fusion.35), calls=%async_computation.1 | async-start | bytes 6291456 | tf_op jit(solution)/shard_map/all_to_all | solution.py:14
  398.0 30.4 %copy-start.3 = (bf16[4,32,768]{2,1,0:T(8,128)(2,1)S(1)}, bf16[4,32,768]{2,1,0:T(8,128)(2,1)}, u32[]{:S(2)}) copy-start(bf16[4,32,768]{2,1,0:T(8,128)(2,1)} %param.13) | copy-start | bytes 589828
  398.0 30.4 %copy-start.4 = (f32[768]{0:T(1024)S(1)}, f32[768]{0:T(1024)}, u32[]{:S(2)}) copy-start(f32[768]{0:T(1024)} %param.14) | copy-start | bytes 9220
  428.4 2.8 copy-start.5
Sparse Core Ops, SparseCore 0:
  12.5 69.9 all-gather.1
  86.8 153.3 all-reduce.2
